TPU v7x, 32 devices: a whole 2x2x4 slice. The times are simulated.
32 devices in a mesh: row: 2 (over x), col: 16 (over z, y, core).
Axes of the slice: x: 2, y: 2, z: 4, core: 2. Of those that a mesh axis runs over, the one named last changes fastest.
Arguments:
- eigvecs: float32 [16384, 4096], P('row', 'col'), may hold values from -6 to 6
- v_panels: float32 [8, 16384, 256], P(None, 'row', 'col'), as said below
- t_panels: float32 [8, 256, 256], P(None, None, 'col'), as said below
Outputs:
- rotated: float32 [16384, 4096], P('row', 'col')
Inputs may be any that keep to these rules, and one draw needn't show every extreme that they name: `v_panels`: in panel k, vector j is zero in rows above k * 256 + j + 1, equals 1 in that row and is dense below it. t_panels[k] is upper triangular and V_k t_panels[k] V_k^T = I minus the product of the panel's 256 Householder reflections, each I - 2 v v^T / (v^T v), taken in the order of j; its diagonal lies in (0, 2].
All inputs are finite; a program needn't handle non-finite values.
Results may differ from a plain program's by a relative error of at most 0.00015.
Values sent between devices are 32-bit elements; how exact they have to be, the bound alone decides.
No kernel may reach another device: no remote copies, remote signals or barrier semaphores. Data moves between devices by JAX's collectives and lax.ppermute only.
A program may use at most 192 MiB of HBM per device.

v0:
```python
import jax
import jax.numpy as jnp
from jax import lax
from jax.sharding import PartitionSpec as P

exact_precision = lax.Precision.HIGHEST


def matmul(left, right):
    return jnp.dot(left, right, preferred_element_type=jnp.float32, precision=exact_precision)


def project(left, right):
    return lax.dot_general(
        left,
        right,
        (((0,), (0,)), ((), ())),
        precision=exact_precision,
        preferred_element_type=jnp.float32,
    )


def local(eigvecs, v_panels, t_panels):
    panels_total = v_panels.shape[0]
    every_v, every_t = (
        lax.all_gather(v_panels, "col", axis=2, tiled=True),
        lax.all_gather(t_panels, "col", axis=2, tiled=True),
    )
    current = eigvecs
    for panel_index in reversed(range(panels_total)):
        vectors = every_v[panel_index]
        factor = every_t[panel_index]
        projected = lax.psum(project(vectors, current), "row")
        current = current - matmul(vectors, matmul(factor, projected))
    return current


def solution(mesh):
    in_specs = (P("row", "col"), P(None, "row", "col"), P(None, None, "col"))
    out_specs = P("row", "col")
    return jax.shard_map(local, mesh=mesh, in_specs=in_specs, out_specs=out_specs, check_vma=False)
```

profile of v0, /device:TPU:0, one launch (start us, length us, event | category | flops | bytes accessed | tf_op | source)
XLA Modules:
  0.0 791.7 jit_solution(15002217065631639125)
XLA Ops:
  6.5 0.7 all-gather.3.cloned.1.call-update
  7.3 0.7 all-gather.5.cloned.1.call-update
  8.1 329.7 %all-gather.3.cloned.1.call-done = f32[8,8192,256]{1,2,0:T(8,128)} async-done(((f32[8,8192,16]{1,2,0:T(8,128)}), f32[8,8192,256]{1,2,0:T(8,128)}) %all-gather.3.cloned.1.call-update) | async-done | bytes 67108880 | tf_op jit(solution)/shard_map/all_gather | solution.py:26
  337.7 11.4 %fusion.8 = f32[256,256]{1,0:T(8,128)} fusion(f32[8192,256]{1,0:T(8,128)} %param.3, f32[8,8192,256]{1,2,0:T(8,128)} %all-gather.3.cloned.1.call-done), kind=kOutput, calls=%fused_computation.24 | convolution fusion | flops 6442450944 | bytes 17039360 | tf_op jit(solution)/shard_map/dot_general | solution.py:14
  349.5 8.9 %copy.4 = f32[8192,256]{0,1:T(8,128)} copy(f32[8192,256]{1,0:T(8,128)} %param.3) | data formatting | bytes 16777216 | tf_op args[0]
  358.4 23.0 %all-gather.5.cloned.1.call-done = f32[8,256,256]{1,2,0:T(8,128)} async-done(((f32[8,256,16]{1,2,0:T(8,128)}), f32[8,256,256]{1,2,0:T(8,128)}) %all-gather.5.cloned.1.call-update) | async-done | bytes 2097168 | tf_op jit(solution)/shard_map/all_gather | solution.py:27
  381.4 24.3 %all-reduce.9.cloned.1.call-done = f32[256,256]{1,0:T(8,128)} async-done(((f32[256,256]{1,0:T(8,128)}), f32[256,256]{1,0:T(8,128)}) %all-reduce.9.cloned.1.call-update) | async-done | bytes 262160 | tf_op jit(solution)/shard_map/psum | solution.py:33
  405.7 1.6 fusion.30
  407.4 11.9 %fusion.7 = f32[8192,256]{0,1:T(8,128)S(1)} fusion(f32[8192,256]{0,1:T(8,128)} %copy.4, f32[256,256]{1,0:T(8,128)S(1)} %fusion.30, f32[8,8192,256]{1,2,0:T(8,128)} %all-gather.3.cloned.1.call-done), kind=kOutput, calls=%fused_computation.15 | convolution fusion | flops 6444548096 | bytes 25427968 | tf_op jit(solution)/shard_map/dot_general | solution.py:10
  419.3 3.4 copy-done
  422.7 10.3 %fusion.22 = f32[256,256]{0,1:T(8,128)} fusion(f32[8192,256]{0,1:T(8,128)S(1)} %fusion.7, f32[8,8192,256]{1,2,0:T(8,128)} %all-gather.3.cloned.1.call-done), kind=kOutput, calls=%fused_computation.38 | convolution fusion | flops 6442450944 | bytes 17039360 | tf_op jit(solution)/shard_map/dot_general | solution.py:14
  433.0 0.4 all-reduce.13.cloned.1.call-start
  433.3 23.1 %all-reduce.11.cloned.1.call-done = f32[256,256]{0,1:T(8,128)} async-done(((f32[256,256]{0,1:T(8,128)}), f32[256,256]{0,1:T(8,128)}) %all-reduce.11.cloned.1.call-update) | async-done | bytes 262160 | tf_op jit(solution)/shard_map/psum | solution.py:33
  456.4 1.3 fusion.29
  457.8 11.9 %fusion.6 = f32[8192,256]{0,1:T(8,128)S(1)} fusion(f32[8192,256]{0,1:T(8,128)} %copy-done, f32[256,256]{1,0:T(8,128)S(1)} %fusion.29, f32[8,8192,256]{1,2,0:T(8,128)} %all-gather.3.cloned.1.call-done), kind=kOutput, calls=%fused_computation.13 | convolution fusion | flops 6444548096 | bytes 25427968 | tf_op jit(solution)/shard_map/dot_general | solution.py:10
  469.7 3.4 copy-done.1
  473.1 10.1 %fusion.21 = f32[256,256]{0,1:T(8,128)} fusion(f32[8192,256]{0,1:T(8,128)S(1)} %fusion.6, f32[8,8192,256]{1,2,0:T(8,128)} %all-gather.3.cloned.1.call-done), kind=kOutput, calls=%fused_computation.37 | convolution fusion | flops 6442450944 | bytes 17039360 | tf_op jit(solution)/shard_map/dot_general | solution.py:14
  483.2 0.6 all-reduce.15.cloned.1.call-start
  483.9 22.8 %all-reduce.13.cloned.1.call-done = f32[256,256]{0,1:T(8,128)} async-done(((f32[256,256]{0,1:T(8,128)}), f32[256,256]{0,1:T(8,128)}) %all-reduce.13.cloned.1.call-update) | async-done | bytes 262160 | tf_op jit(solution)/shard_map/psum | solution.py:33
  506.7 1.3 fusion.28
  508.0 11.9 %fusion.5 = f32[8192,256]{0,1:T(8,128)S(1)} fusion(f32[8192,256]{0,1:T(8,128)} %copy-done.1, f32[256,256]{1,0:T(8,128)S(1)} %fusion.28, f32[8,8192,256]{1,2,0:T(8,128)} %all-gather.3.cloned.1.call-done), kind=kOutput, calls=%fused_computation.11 | convolution fusion | flops 6444548096 | bytes 25427968 | tf_op jit(solution)/shard_map/dot_general | solution.py:10
  519.9 3.4 copy-done.2
  523.3 10.1 %fusion.20 = f32[256,256]{0,1:T(8,128)} fusion(f32[8192,256]{0,1:T(8,128)S(1)} %fusion.5, f32[8,8192,256]{1,2,0:T(8,128)} %all-gather.3.cloned.1.call-done), kind=kOutput, calls=%fused_computation.36 | convolution fusion | flops 6442450944 | bytes 17039360 | tf_op jit(solution)/shard_map/dot_general | solution.py:14
  533.7 23.2 %all-reduce.15.cloned.1.call-done = f32[256,256]{0,1:T(8,128)} async-done(((f32[256,256]{0,1:T(8,128)}), f32[256,256]{0,1:T(8,128)}) %all-reduce.15.cloned.1.call-update) | async-done | bytes 262160 | tf_op jit(solution)/shard_map/psum | solution.py:33
  556.9 1.3 fusion.27
  558.3 11.9 %fusion.4 = f32[8192,256]{0,1:T(8,128)S(1)} fusion(f32[8192,256]{0,1:T(8,128)} %copy-done.2, f32[256,256]{1,0:T(8,128)S(1)} %fusion.27, f32[8,8192,256]{1,2,0:T(8,128)} %all-gather.3.cloned.1.call-done), kind=kOutput, calls=%fused_computation.9 | convolution fusion | flops 6444548096 | bytes 25427968 | tf_op jit(solution)/shard_map/dot_general | solution.py:10
  570.2 3.4 copy-done.3
  573.6 10.1 %fusion.19 = f32[256,256]{0,1:T(8,128)} fusion(f32[8192,256]{0,1:T(8,128)S(1)} %fusion.4, f32[8,8192,256]{1,2,0:T(8,128)} %all-gather.3.cloned.1.call-done), kind=kOutput, calls=%fused_computation.35 | convolution fusion | flops 6442450944 | bytes 17039360 | tf_op jit(solution)/shard_map/dot_general | solution.py:14
  584.0 23.2 %all-reduce.17.cloned.1.call-done = f32[256,256]{0,1:T(8,128)} async-done(((f32[256,256]{0,1:T(8,128)}), f32[256,256]{0,1:T(8,128)}) %all-reduce.17.cloned.1.call-update) | async-done | bytes 262160 | tf_op jit(solution)/shard_map/psum | solution.py:33
  607.2 1.3 fusion.26
  608.5 11.9 %fusion.3 = f32[8192,256]{0,1:T(8,128)S(1)} fusion(f32[8192,256]{0,1:T(8,128)} %copy-done.3, f32[256,256]{1,0:T(8,128)S(1)} %fusion.26, f32[8,8192,256]{1,2,0:T(8,128)} %all-gather.3.cloned.1.call-done), kind=kOutput, calls=%fused_computation.7 | convolution fusion | flops 6444548096 | bytes 25427968 | tf_op jit(solution)/shard_map/dot_general | solution.py:10
  620.4 3.4 copy-done.4
  623.8 10.1 %fusion.18 = f32[256,256]{0,1:T(8,128)} fusion(f32[8192,256]{0,1:T(8,128)S(1)} %fusion.3, f32[8,8192,256]{1,2,0:T(8,128)} %all-gather.3.cloned.1.call-done), kind=kOutput, calls=%fused_computation.34 | convolution fusion | flops 6442450944 | bytes 17039360 | tf_op jit(solution)/shard_map/dot_general | solution.py:14
  634.3 23.2 %all-reduce.19.cloned.1.call-done = f32[256,256]{0,1:T(8,128)} async-done(((f32[256,256]{0,1:T(8,128)}), f32[256,256]{0,1:T(8,128)}) %all-reduce.19.cloned.1.call-update) | async-done | bytes 262160 | tf_op jit(solution)/shard_map/psum | solution.py:33
  657.4 1.3 fusion.25
  658.8 11.9 %fusion.2 = f32[8192,256]{0,1:T(8,128)S(1)} fusion(f32[8192,256]{0,1:T(8,128)} %copy-done.4, f32[256,256]{1,0:T(8,128)S(1)} %fusion.25, f32[8,8192,256]{1,2,0:T(8,128)} %all-gather.3.cloned.1.call-done), kind=kOutput, calls=%fused_computation.5 | convolution fusion | flops 6444548096 | bytes 25427968 | tf_op jit(solution)/shard_map/dot_general | solution.py:10
  670.7 3.4 copy-done.5
  674.1 10.1 %fusion.17 = f32[256,256]{0,1:T(8,128)} fusion(f32[8192,256]{0,1:T(8,128)S(1)} %fusion.2, f32[8,8192,256]{1,2,0:T(8,128)} %all-gather.3.cloned.1.call-done), kind=kOutput, calls=%fused_computation.33 | convolution fusion | flops 6442450944 | bytes 17039360 | tf_op jit(solution)/shard_map/dot_general | solution.py:14
  684.2 0.5 all-reduce.23.cloned.1.call-start
  684.7 22.9 %all-reduce.21.cloned.1.call-done = f32[256,256]{0,1:T(8,128)} async-done(((f32[256,256]{0,1:T(8,128)}), f32[256,256]{0,1:T(8,128)}) %all-reduce.21.cloned.1.call-update) | async-done | bytes 262160 | tf_op jit(solution)/shard_map/psum | solution.py:33
  707.7 1.3 fusion.24
  709.0 11.9 %fusion.1 = f32[8192,256]{0,1:T(8,128)S(1)} fusion(f32[8192,256]{0,1:T(8,128)} %copy-done.5, f32[256,256]{1,0:T(8,128)S(1)} %fusion.24, f32[8,8192,256]{1,2,0:T(8,128)} %all-gather.3.cloned.1.call-done), kind=kOutput, calls=%fused_computation.3 | convolution fusion | flops 6444548096 | bytes 25427968 | tf_op jit(solution)/shard_map/dot_general | solution.py:10
  720.9 3.4 copy-done.6
  724.3 10.1 %fusion.16 = f32[256,256]{0,1:T(8,128)} fusion(f32[8192,256]{0,1:T(8,128)S(1)} %fusion.1, f32[8,8192,256]{1,2,0:T(8,128)} %all-gather.3.cloned.1.call-done), kind=kOutput, calls=%fused_computation.32 | convolution fusion | flops 6442450944 | bytes 17039360 | tf_op jit(solution)/shard_map/dot_general | solution.py:14
  734.5 23.5 %all-reduce.23.cloned.1.call-done = f32[256,256]{0,1:T(8,128)} async-done(((f32[256,256]{0,1:T(8,128)}), f32[256,256]{0,1:T(8,128)}) %all-reduce.23.cloned.1.call-update) | async-done | bytes 262160 | tf_op jit(solution)/shard_map/psum | solution.py:33
  757.9 1.3 fusion.23
  759.3 16.4 %fusion = f32[8192,256]{0,1:T(8,128)} fusion(f32[8192,256]{0,1:T(8,128)} %copy-done.6, f32[256,256]{1,0:T(8,128)S(1)} %fusion.23, f32[8,8192,256]{1,2,0:T(8,128)} %all-gather.3.cloned.1.call-done), kind=kOutput, calls=%fused_computation.1 | convolution fusion | flops 6444548096 | bytes 25427968 | tf_op jit(solution)/shard_map/dot_general | solution.py:10
  775.7 9.0 %copy.5 = f32[8192,256]{1,0:T(8,128)} copy(f32[8192,256]{0,1:T(8,128)} %fusion) | data formatting | bytes 16777216 | tf_op jit(solution)/shard_map/sub | solution.py:34
  (24 shorter events, 1.3 us)
Async XLA Ops:
  6.5 331.2 %all-gather.3.cloned.1.call-start = ((), (), s32[]{:S(2)}) async-start(), calls=%async_computation | async-start | bytes 71303168 | tf_op jit(solution)/shard_map/all_gather | solution.py:26
  7.3 374.2 %all-gather.5.cloned.1.call-start = ((), (), s32[]{:S(2)}) async-start(), calls=%async_computation.2 | async-start | bytes 2228224 | tf_op jit(solution)/shard_map/all_gather | solution.py:27
  8.0 397.7 %all-reduce.9.cloned.1.call-start = ((), (), s32[]{:S(2)}) async-start(), calls=%async_computation.1 | async-start | bytes 524288 | tf_op jit(solution)/shard_map/psum | solution.py:33
  349.1 107.3 %all-reduce.11.cloned.1.call-start = ((), (), s32[]{:S(2)}) async-start(), calls=%async_computation.3 | async-start | bytes 524288 | tf_op jit(solution)/shard_map/psum | solution.py:33
  419.3 3.4 copy-start
  422.7 33.8 %copy-start.7 = (f32[8,256,256]{1,2,0:T(8,128)S(1)}, f32[8,256,256]{1,2,0:T(8,128)}, u32[]{:S(2)}) copy-start(f32[8,256,256]{1,2,0:T(8,128)} %all-gather.5.cloned.1.call-done) | copy-start | bytes 6291460
  433.0 73.7 %all-reduce.13.cloned.1.call-start = ((), (), s32[]{:S(2)}) async-start(), calls=%async_computation.4 | async-start | bytes 524288 | tf_op jit(solution)/shard_map/psum | solution.py:33
  469.7 3.4 copy-start.1
  483.2 73.7 %all-reduce.15.cloned.1.call-start = ((), (), s32[]{:S(2)}) async-start(), calls=%async_computation.5 | async-start | bytes 524288 | tf_op jit(solution)/shard_map/psum | solution.py:33
  519.9 3.4 copy-start.2
  533.5 73.7 %all-reduce.17.cloned.1.call-start = ((), (), s32[]{:S(2)}) async-start(), calls=%async_computation.6 | async-start | bytes 524288 | tf_op jit(solution)/shard_map/psum | solution.py:33
  570.2 3.4 copy-start.3
  583.7 73.7 %all-reduce.19.cloned.1.call-start = ((), (), s32[]{:S(2)}) async-start(), calls=%async_computation.7 | async-start | bytes 524288 | tf_op jit(solution)/shard_map/psum | solution.py:33
  620.4 3.4 copy-start.4
  634.0 73.7 %all-reduce.21.cloned.1.call-start = ((), (), s32[]{:S(2)}) async-start(), calls=%async_computation.8 | async-start | bytes 524288 | tf_op jit(solution)/shard_map/psum | solution.py:33
  670.7 3.4 copy-start.5
  684.2 73.7 %all-reduce.23.cloned.1.call-start = ((), (), s32[]{:S(2)}) async-start(), calls=%async_computation.9 | async-start | bytes 524288 | tf_op jit(solution)/shard_map/psum | solution.py:33
  720.9 3.4 copy-start.6
Sparse Core Ops, SparseCore 0:
  8.9 328.7 all-gather.2
  339.9 41.4 all-gather.4
  383.7 22.0 all-reduce.8
  433.1 23.2 all-reduce.10
  483.3 23.2 all-reduce.12
  533.6 23.2 all-reduce.14
  583.8 23.2 all-reduce.16
  634.1 23.2 all-reduce.18
  684.3 23.2 all-reduce.20
  734.6 23.2 all-reduce.22
where the time goes:
time: 796 us; the launch traced here: 792 us
  waiting for transfers between devices  540 us (68%)
  matrix products  193 us (24%)
  local copies, waits for them, and re-layouts  41.6 us (5%)
  between operations  13.9 us (2%)
    all_gather x1, waiting for transfers between devices, local(): lax.all_gather(v_panels, 'col', axis=2, tiled=True)  330 us
    psum x8, waiting for transfers between devices, local(): projected = lax.psum(project(vectors, current), 'row')  186 us
    dot_general x16, matrix products, matmul(): jnp.dot(left, right, preferred_element_type=jnp.float32, precision=exact_...  111 us
    dot_general x8, matrix products, project(): lax.dot_general(left, right, (((0,), (0,)), ((), ())), precision=exact_pr...  82.4 us
    unnamed x17, local copies, waits for them, and re-layouts  32.7 us
    all_gather x1, waiting for transfers between devices, local(): lax.all_gather(t_panels, 'col', axis=2, tiled=True)  23 us
  transfers between devices with their start and end apart: 10, of which 10 were waited for; matrix products, arithmetic and copies ran while one was open for 3% of the time, Pallas kernels for 0%

commit v1 on v0

v1 whole, which is shorter than its diff:
```python
import jax
import jax.numpy as jnp
from jax import lax
from jax.sharding import PartitionSpec as P

three_pass = lax.Precision.HIGH
GROUPS = (2, 2, 2, 1, 1)


def dot(left, right, contract):
    return lax.dot_general(
        left, right, (contract, ((), ())), precision=three_pass, preferred_element_type=jnp.float32
    )


def row_sum(partial, rows):
    if rows == 2:
        return partial + lax.ppermute(partial, "row", [(0, 1), (1, 0)])
    return lax.psum(partial, "row")


def group_sizes(panels_total):
    sizes = []
    left = panels_total
    for size in GROUPS:
        size = min(size, left)
        if size:
            sizes.append(size)
        left -= size
    while left:
        sizes.append(1)
        left -= 1
    return sizes


def solution(mesh):
    rows = mesh.shape["row"]

    def local(eigvecs, v_panels, t_panels):
        panels_total, height, _ = v_panels.shape
        groups = []
        high = panels_total
        for size in group_sizes(panels_total):
            low = high - size
            packed = jnp.concatenate([v_panels[low:high], t_panels[low:high]], axis=1)
            groups.append((low, high, lax.all_gather(packed, "col", axis=2, tiled=True)))
            high = low
        current = eigvecs
        for low, high, every in groups:
            for panel_index in reversed(range(low, high)):
                vectors = every[panel_index - low, :height]
                factor = every[panel_index - low, height:]
                projected = row_sum(dot(vectors, current, ((0,), (0,))), rows)
                scaled = dot(factor, projected, ((1,), (0,)))
                current = current - dot(vectors, scaled, ((1,), (0,)))
        return current

    in_specs = (P("row", "col"), P(None, "row", "col"), P(None, None, "col"))
    out_specs = P("row", "col")
    return jax.shard_map(local, mesh=mesh, in_specs=in_specs, out_specs=out_specs, check_vma=False)
```

time: 796 us -> 490 us (0.62)
  waiting for transfers between devices: 540 us -> 267 us
  local copies, waits for them, and re-layouts: 41.6 us -> 4.9 us
  matrix products: 193 us -> 178 us
  starting transfers between devices: 2.68 us -> 12.4 us
    psum x8 -> x0, waiting for transfers between devices: 186 us -> none  [local(): projected = lax.psum(project(vectors, current), 'row')]
    all_gather x2 -> x5, waiting for transfers between devices: 353 us -> 213 us  [local(): lax.all_gather(packed, 'col', axis=2, tiled=True)]
    ppermute x0 -> x8, waiting for transfers between devices: none -> 53.7 us  [row_sum(): return partial + lax.ppermute(partial, 'row', [(0, 1), (1, 0)])]
    unnamed x17 -> x12, local copies, waits for them, and re-layouts: 32.7 us -> 0.02 us
    dot_general x24, matrix products: 193 us -> 178 us  [dot(): lax.dot_general(left, right, (contract, ((), ())), precision=three_pass,...]
    ppermute x0 -> x8, starting transfers between devices: none -> 12.3 us  [row_sum(): return partial + lax.ppermute(partial, 'row', [(0, 1), (1, 0)])]
    sub x1 -> x0, local copies, waits for them, and re-layouts: 8.99 us -> none  [local(): current = current - matmul(vectors, matmul(factor, projected))]
  transfers between devices with their start and end apart: 10 -> 13, of which waited for: 10 -> 13; matrix products, arithmetic and copies ran while one was open for 3% -> 34% of each run, Pallas kernels for 0% -> 0%
where the time goes in v1:
time: 490 us; the launch traced here: 481 us
  waiting for transfers between devices  267 us (54%)
  matrix products  178 us (36%)
  between operations  13.8 us (3%)
  starting transfers between devices  12.4 us (3%)
  local copies, waits for them, and re-layouts  4.9 us (1%)
    all_gather x5, waiting for transfers between devices, local(): lax.all_gather(packed, 'col', axis=2, tiled=True)  213 us
    dot_general x24, matrix products, dot(): lax.dot_general(left, right, (contract, ((), ())), precision=three_pass,...  178 us
    ppermute x8, waiting for transfers between devices, row_sum(): return partial + lax.ppermute(partial, 'row', [(0, 1), (1, 0)])  53.7 us
    ppermute x8, starting transfers between devices, row_sum(): return partial + lax.ppermute(partial, 'row', [(0, 1), (1, 0)])  12.3 us
  transfers between devices with their start and end apart: 13, of which 13 were waited for; matrix products, arithmetic and copies ran while one was open for 34% of the time, Pallas kernels for 0%

profile of v1, /device:TPU:0, one launch (start us, length us, event | category | flops | bytes accessed | tf_op | source)
XLA Modules:
  0.0 480.7 jit_solution(1358471341085149776)
XLA Ops:
  6.5 2.1 fusion.25
  9.4 1.1 pad_maximum_fusion
  10.5 1.0 pad_maximum_fusion.1
  11.6 1.1 pad_maximum_fusion.2
  13.5 1.3 fusion.24
  16.6 88.3 %all-gather.6.cloned.1.call-done = f32[2,8448,256]{1,2,0:T(8,128)} async-done(((f32[2,8448,16]{1,2,0:T(8,128)}), f32[2,8448,256]{1,2,0:T(8,128)}) %all-gather.6.cloned.1.call-update) | async-done | bytes 17301520 | tf_op jit(solution)/shard_map/all_gather | solution.py:46
  104.8 9.3 %fusion = f32[256,256]{1,0:T(8,128)S(1)} fusion(f32[8192,256]{1,0:T(8,128)} %param.3, f32[2,8448,256]{1,2,0:T(8,128)} %all-gather.6.cloned.1.call-done), kind=kOutput, calls=%fused_computation.16 | convolution fusion | flops 3221225472 | bytes 17039360 | tf_op jit(solution)/shard_map/dot_general | solution.py:11
  114.1 1.5 collective-permute-start
  115.7 7.0 %collective-permute-done = f32[256,256]{1,0:T(8,128)S(1)} collective-permute-done((f32[256,256]{1,0:T(8,128)S(1)}, f32[256,256]{1,0:T(8,128)S(1)}, u32[]{:S(2)}, u32[]{:S(2)}) %collective-permute-start) | collective-permute-done | bytes 262176 | tf_op jit(solution)/shard_map/ppermute | solution.py:18
  122.7 1.3 fusion.15
  124.0 13.4 %convolution_subtract_fusion.7 = f32[8192,256]{1,0:T(8,128)S(1)} fusion(f32[8192,256]{1,0:T(8,128)} %param.3, f32[256,256]{1,0:T(8,128)S(1)} %fusion.15, f32[2,8448,256]{1,2,0:T(8,128)} %all-gather.6.cloned.1.call-done), kind=kOutput, calls=%fused_computation.7 | convolution fusion | flops 3223322624 | bytes 25427968 | tf_op jit(solution)/shard_map/dot_general | solution.py:11
  137.4 8.5 %fusion.1 = f32[256,256]{1,0:T(8,128)S(1)} fusion(f32[8192,256]{1,0:T(8,128)S(1)} %convolution_subtract_fusion.7, f32[2,8448,256]{1,2,0:T(8,128)} %all-gather.6.cloned.1.call-done), kind=kOutput, calls=%fused_computation.17 | convolution fusion | flops 3221225472 | bytes 17039360 | tf_op jit(solution)/shard_map/dot_general | solution.py:11
  145.9 1.5 collective-permute-start.1
  147.4 6.2 %collective-permute-done.1 = f32[256,256]{1,0:T(8,128)S(1)} collective-permute-done((f32[256,256]{1,0:T(8,128)S(1)}, f32[256,256]{1,0:T(8,128)S(1)}, u32[]{:S(2)}, u32[]{:S(2)}) %collective-permute-start.1) | collective-permute-done | bytes 262176 | tf_op jit(solution)/shard_map/ppermute | solution.py:18
  153.7 1.4 fusion.14
  155.0 14.1 %convolution_subtract_fusion.6 = f32[8192,256]{1,0:T(8,128)} fusion(f32[8192,256]{1,0:T(8,128)S(1)} %convolution_subtract_fusion.7, f32[256,256]{1,0:T(8,128)S(1)} %fusion.14, f32[2,8448,256]{1,2,0:T(8,128)} %all-gather.6.cloned.1.call-done), kind=kOutput, calls=%fused_computation.6 | convolution fusion | flops 3223322624 | bytes 25427968 | tf_op jit(solution)/shard_map/dot_general | solution.py:11
  169.2 28.7 %all-gather.8.cloned.1.call-done = f32[2,8448,256]{1,2,0:T(8,128)} async-done(((f32[2,8448,16]{1,2,0:T(8,128)}), f32[2,8448,256]{1,2,0:T(8,128)}) %all-gather.8.cloned.1.call-update) | async-done | bytes 17301520 | tf_op jit(solution)/shard_map/all_gather | solution.py:46
  197.9 10.3 %fusion.2 = f32[256,256]{1,0:T(8,128)S(1)} fusion(f32[8192,256]{1,0:T(8,128)} %convolution_subtract_fusion.6, f32[2,8448,256]{1,2,0:T(8,128)} %all-gather.8.cloned.1.call-done), kind=kOutput, calls=%fused_computation.18 | convolution fusion | flops 3221225472 | bytes 17039360 | tf_op jit(solution)/shard_map/dot_general | solution.py:11
  208.2 1.5 collective-permute-start.2
  209.8 7.0 %collective-permute-done.2 = f32[256,256]{1,0:T(8,128)S(1)} collective-permute-done((f32[256,256]{1,0:T(8,128)S(1)}, f32[256,256]{1,0:T(8,128)S(1)}, u32[]{:S(2)}, u32[]{:S(2)}) %collective-permute-start.2) | collective-permute-done | bytes 262176 | tf_op jit(solution)/shard_map/ppermute | solution.py:18
  216.8 1.3 fusion.13
  218.1 9.7 %convolution_subtract_fusion.5 = f32[8192,256]{1,0:T(8,128)S(1)} fusion(f32[8192,256]{1,0:T(8,128)S(1)} %copy-done.2, f32[256,256]{1,0:T(8,128)S(1)} %fusion.13, f32[2,8448,256]{1,2,0:T(8,128)} %all-gather.8.cloned.1.call-done), kind=kOutput, calls=%fused_computation.5 | convolution fusion | flops 3223322624 | bytes 25427968 | tf_op jit(solution)/shard_map/dot_general | solution.py:11
  227.8 8.4 %fusion.3 = f32[256,256]{1,0:T(8,128)S(1)} fusion(f32[8192,256]{1,0:T(8,128)S(1)} %convolution_subtract_fusion.5, f32[2,8448,256]{1,2,0:T(8,128)} %all-gather.8.cloned.1.call-done), kind=kOutput, calls=%fused_computation.19 | convolution fusion | flops 3221225472 | bytes 17039360 | tf_op jit(solution)/shard_map/dot_general | solution.py:11
  236.2 1.5 collective-permute-start.3
  237.7 6.3 %collective-permute-done.3 = f32[256,256]{1,0:T(8,128)S(1)} collective-permute-done((f32[256,256]{1,0:T(8,128)S(1)}, f32[256,256]{1,0:T(8,128)S(1)}, u32[]{:S(2)}, u32[]{:S(2)}) %collective-permute-start.3) | collective-permute-done | bytes 262176 | tf_op jit(solution)/shard_map/ppermute | solution.py:18
  244.0 1.3 fusion.12
  245.4 14.2 %convolution_subtract_fusion.4 = f32[8192,256]{1,0:T(8,128)} fusion(f32[8192,256]{1,0:T(8,128)S(1)} %convolution_subtract_fusion.5, f32[256,256]{1,0:T(8,128)S(1)} %fusion.12, f32[2,8448,256]{1,2,0:T(8,128)} %all-gather.8.cloned.1.call-done), kind=kOutput, calls=%fused_computation.4 | convolution fusion | flops 3223322624 | bytes 25427968 | tf_op jit(solution)/shard_map/dot_general | solution.py:11
  259.5 31.4 %all-gather.10.cloned.1.call-done = f32[2,8448,256]{1,2,0:T(8,128)} async-done(((f32[2,8448,16]{1,2,0:T(8,128)}), f32[2,8448,256]{1,2,0:T(8,128)}) %all-gather.10.cloned.1.call-update) | async-done | bytes 17301520 | tf_op jit(solution)/shard_map/all_gather | solution.py:46
  291.0 10.3 %fusion.4 = f32[256,256]{1,0:T(8,128)S(1)} fusion(f32[8192,256]{1,0:T(8,128)} %convolution_subtract_fusion.4, f32[2,8448,256]{1,2,0:T(8,128)} %all-gather.10.cloned.1.call-done), kind=kOutput, calls=%fused_computation.20 | convolution fusion | flops 3221225472 | bytes 17039360 | tf_op jit(solution)/shard_map/dot_general | solution.py:11
  301.3 1.5 collective-permute-start.4
  302.8 7.0 %collective-permute-done.4 = f32[256,256]{1,0:T(8,128)S(1)} collective-permute-done((f32[256,256]{1,0:T(8,128)S(1)}, f32[256,256]{1,0:T(8,128)S(1)}, u32[]{:S(2)}, u32[]{:S(2)}) %collective-permute-start.4) | collective-permute-done | bytes 262176 | tf_op jit(solution)/shard_map/ppermute | solution.py:18
  309.8 1.3 fusion.11
  311.2 9.9 %convolution_subtract_fusion.3 = f32[8192,256]{1,0:T(8,128)S(1)} fusion(f32[8192,256]{1,0:T(8,128)S(1)} %copy-done.3, f32[256,256]{1,0:T(8,128)S(1)} %fusion.11, f32[2,8448,256]{1,2,0:T(8,128)} %all-gather.10.cloned.1.call-done), kind=kOutput, calls=%fused_computation.3 | convolution fusion | flops 3223322624 | bytes 25427968 | tf_op jit(solution)/shard_map/dot_general | solution.py:11
  321.0 8.4 %fusion.5 = f32[256,256]{1,0:T(8,128)S(1)} fusion(f32[8192,256]{1,0:T(8,128)S(1)} %convolution_subtract_fusion.3, f32[2,8448,256]{1,2,0:T(8,128)} %all-gather.10.cloned.1.call-done), kind=kOutput, calls=%fused_computation.21 | convolution fusion | flops 3221225472 | bytes 17039360 | tf_op jit(solution)/shard_map/dot_general | solution.py:11
  329.4 1.5 collective-permute-start.5
  331.0 6.2 %collective-permute-done.5 = f32[256,256]{1,0:T(8,128)S(1)} collective-permute-done((f32[256,256]{1,0:T(8,128)S(1)}, f32[256,256]{1,0:T(8,128)S(1)}, u32[]{:S(2)}, u32[]{:S(2)}) %collective-permute-start.5) | collective-permute-done | bytes 262176 | tf_op jit(solution)/shard_map/ppermute | solution.py:18
  337.2 1.3 fusion.10
  338.6 14.0 %convolution_subtract_fusion.2 = f32[8192,256]{1,0:T(8,128)} fusion(f32[8192,256]{1,0:T(8,128)S(1)} %convolution_subtract_fusion.3, f32[256,256]{1,0:T(8,128)S(1)} %fusion.10, f32[2,8448,256]{1,2,0:T(8,128)} %all-gather.10.cloned.1.call-done), kind=kOutput, calls=%fused_computation.2 | convolution fusion | flops 3223322624 | bytes 25427968 | tf_op jit(solution)/shard_map/dot_general | solution.py:11
  352.5 16.5 %all-gather.12.cloned.1.call-done = f32[1,8448,256]{1,2,0:T(8,128)} async-done(((f32[1,8448,16]{1,2,0:T(8,128)}), f32[1,8448,256]{1,2,0:T(8,128)}) %all-gather.12.cloned.1.call-update) | async-done | bytes 8650768 | tf_op jit(solution)/shard_map/all_gather | solution.py:46
  369.1 9.5 %fusion.6 = f32[256,256]{1,0:T(8,128)S(1)} fusion(f32[8192,256]{1,0:T(8,128)} %convolution_subtract_fusion.2, f32[1,8448,256]{1,2,0:T(8,128)} %all-gather.12.cloned.1.call-done), kind=kOutput, calls=%fused_computation.22 | convolution fusion | flops 3221225472 | bytes 17039360 | tf_op jit(solution)/shard_map/dot_general | solution.py:11
  378.6 1.5 collective-permute-start.6
  380.1 7.0 %collective-permute-done.6 = f32[256,256]{1,0:T(8,128)S(1)} collective-permute-done((f32[256,256]{1,0:T(8,128)S(1)}, f32[256,256]{1,0:T(8,128)S(1)}, u32[]{:S(2)}, u32[]{:S(2)}) %collective-permute-start.6) | collective-permute-done | bytes 262176 | tf_op jit(solution)/shard_map/ppermute | solution.py:18
  387.6 9.8 %convolution_subtract_fusion.1 = f32[8192,256]{1,0:T(8,128)} fusion(f32[8192,256]{1,0:T(8,128)S(1)} %copy-done, f32[256,256]{1,0:T(8,128)S(1)} %fusion.9, f32[1,8448,256]{1,2,0:T(8,128)S(1)} %copy-done.5), kind=kOutput, calls=%fused_computation.1 | convolution fusion | flops 3223322624 | bytes 25427968 | tf_op jit(solution)/shard_map/dot_general | solution.py:11
  397.4 48.4 %all-gather.14.cloned.1.call-done = f32[1,8448,256]{1,2,0:T(8,128)} async-done(((f32[1,8448,16]{1,2,0:T(8,128)}), f32[1,8448,256]{1,2,0:T(8,128)}) %all-gather.14.cloned.1.call-update) | async-done | bytes 8650768 | tf_op jit(solution)/shard_map/all_gather | solution.py:46
  445.7 9.5 %fusion.7 = f32[256,256]{1,0:T(8,128)S(1)} fusion(f32[8192,256]{1,0:T(8,128)} %convolution_subtract_fusion.1, f32[1,8448,256]{1,2,0:T(8,128)} %all-gather.14.cloned.1.call-done), kind=kOutput, calls=%fused_computation.23 | convolution fusion | flops 3221225472 | bytes 17039360 | tf_op jit(solution)/shard_map/dot_general | solution.py:11
  455.3 1.5 collective-permute-start.7
  456.8 7.0 %collective-permute-done.7 = f32[256,256]{1,0:T(8,128)S(1)} collective-permute-done((f32[256,256]{1,0:T(8,128)S(1)}, f32[256,256]{1,0:T(8,128)S(1)}, u32[]{:S(2)}, u32[]{:S(2)}) %collective-permute-start.7) | collective-permute-done | bytes 262176 | tf_op jit(solution)/shard_map/ppermute | solution.py:18
  464.2 9.5 %convolution_subtract_fusion = f32[8192,256]{1,0:T(8,128)} fusion(f32[8192,256]{1,0:T(8,128)S(1)} %copy-done.1, f32[256,256]{1,0:T(8,128)S(1)} %fusion.8, f32[1,8448,256]{1,2,0:T(8,128)S(1)} %copy-done.4), kind=kOutput, calls=%fused_computation | convolution fusion | flops 3223322624 | bytes 25427968 | tf_op jit(solution)/shard_map/dot_general | solution.py:11
  (28 shorter events, 4.3 us)
Async XLA Ops:
  6.5 98.3 %all-gather.6.cloned.1.call-start = ((), (), s32[]{:S(2)}) async-start(), calls=%async_computation | async-start | bytes 18382848 | tf_op jit(solution)/shard_map/all_gather | solution.py:46
  10.5 187.4 %all-gather.8.cloned.1.call-start = ((), (), s32[]{:S(2)}) async-start(), calls=%async_computation.1 | async-start | bytes 18382848 | tf_op jit(solution)/shard_map/all_gather | solution.py:46
  11.6 279.4 %all-gather.10.cloned.1.call-start = ((), (), s32[]{:S(2)}) async-start(), calls=%async_computation.2 | async-start | bytes 18382848 | tf_op jit(solution)/shard_map/all_gather | solution.py:46
  12.7 356.3 %all-gather.12.cloned.1.call-start = ((), (), s32[]{:S(2)}) async-start(), calls=%async_computation.3 | async-start | bytes 9191424 | tf_op jit(solution)/shard_map/all_gather | solution.py:46
  15.7 430.1 %all-gather.14.cloned.1.call-start = ((), (), s32[]{:S(2)}) async-start(), calls=%async_computation.4 | async-start | bytes 9191424 | tf_op jit(solution)/shard_map/all_gather | solution.py:46
  114.1 8.5 %collective-permute-start = (f32[256,256]{1,0:T(8,128)S(1)}, f32[256,256]{1,0:T(8,128)S(1)}, u32[]{:S(2)}, u32[]{:S(2)}) collective-permute-start(f32[256,256]{1,0:T(8,128)S(1)} %fusion), channel_id=1, source_target_pairs={{0,16},{16,0},{1,17},{17,1},{2,18},{18,2},{3,19},{19,3},{4,20},{20... | collective-permute-start | bytes 786440 | tf_op jit(solution)/shard_map/ppermute | solution.py:18
  145.9 7.8 %collective-permute-start.1 = (f32[256,256]{1,0:T(8,128)S(1)}, f32[256,256]{1,0:T(8,128)S(1)}, u32[]{:S(2)}, u32[]{:S(2)}) collective-permute-start(f32[256,256]{1,0:T(8,128)S(1)} %fusion.1), channel_id=1, source_target_pairs={{0,16},{16,0},{1,17},{17,1},{2,18},{18,2},{3,19},{19,3},{4,20},{20... | collective-permute-start | bytes 786440 | tf_op jit(solution)/shard_map/ppermute | solution.py:18
  197.9 20.2 %copy-start.2 = (f32[8192,256]{1,0:T(8,128)S(1)}, f32[8192,256]{1,0:T(8,128)}, u32[]{:S(2)}) copy-start(f32[8192,256]{1,0:T(8,128)} %convolution_subtract_fusion.6) | copy-start | bytes 25165828
  208.2 8.5 %collective-permute-start.2 = (f32[256,256]{1,0:T(8,128)S(1)}, f32[256,256]{1,0:T(8,128)S(1)}, u32[]{:S(2)}, u32[]{:S(2)}) collective-permute-start(f32[256,256]{1,0:T(8,128)S(1)} %fusion.2), channel_id=1, source_target_pairs={{0,16},{16,0},{1,17},{17,1},{2,18},{18,2},{3,19},{19,3},{4,20},{20... | collective-permute-start | bytes 786440 | tf_op jit(solution)/shard_map/ppermute | solution.py:18
  236.2 7.8 %collective-permute-start.3 = (f32[256,256]{1,0:T(8,128)S(1)}, f32[256,256]{1,0:T(8,128)S(1)}, u32[]{:S(2)}, u32[]{:S(2)}) collective-permute-start(f32[256,256]{1,0:T(8,128)S(1)} %fusion.3), channel_id=1, source_target_pairs={{0,16},{16,0},{1,17},{17,1},{2,18},{18,2},{3,19},{19,3},{4,20},{20... | collective-permute-start | bytes 786440 | tf_op jit(solution)/shard_map/ppermute | solution.py:18
  291.0 20.2 %copy-start.3 = (f32[8192,256]{1,0:T(8,128)S(1)}, f32[8192,256]{1,0:T(8,128)}, u32[]{:S(2)}) copy-start(f32[8192,256]{1,0:T(8,128)} %convolution_subtract_fusion.4) | copy-start | bytes 25165828
  301.3 8.5 %collective-permute-start.4 = (f32[256,256]{1,0:T(8,128)S(1)}, f32[256,256]{1,0:T(8,128)S(1)}, u32[]{:S(2)}, u32[]{:S(2)}) collective-permute-start(f32[256,256]{1,0:T(8,128)S(1)} %fusion.4), channel_id=1, source_target_pairs={{0,16},{16,0},{1,17},{17,1},{2,18},{18,2},{3,19},{19,3},{4,20},{20... | collective-permute-start | bytes 786440 | tf_op jit(solution)/shard_map/ppermute | solution.py:18
  329.4 7.8 %collective-permute-start.5 = (f32[256,256]{1,0:T(8,128)S(1)}, f32[256,256]{1,0:T(8,128)S(1)}, u32[]{:S(2)}, u32[]{:S(2)}) collective-permute-start(f32[256,256]{1,0:T(8,128)S(1)} %fusion.5), channel_id=1, source_target_pairs={{0,16},{16,0},{1,17},{17,1},{2,18},{18,2},{3,19},{19,3},{4,20},{20... | collective-permute-start | bytes 786440 | tf_op jit(solution)/shard_map/ppermute | solution.py:18
  369.1 18.1 %copy-start.5 = (f32[1,8448,256]{1,2,0:T(8,128)S(1)}, f32[1,8448,256]{1,2,0:T(8,128)}, u32[]{:S(2)}) copy-start(f32[1,8448,256]{1,2,0:T(8,128)} %all-gather.12.cloned.1.call-done) | copy-start | bytes 25952260
  369.1 18.5 %copy-start = (f32[8192,256]{1,0:T(8,128)S(1)}, f32[8192,256]{1,0:T(8,128)}, u32[]{:S(2)}) copy-start(f32[8192,256]{1,0:T(8,128)} %convolution_subtract_fusion.2) | copy-start | bytes 25165828
  378.6 8.5 %collective-permute-start.6 = (f32[256,256]{1,0:T(8,128)S(1)}, f32[256,256]{1,0:T(8,128)S(1)}, u32[]{:S(2)}, u32[]{:S(2)}) collective-permute-start(f32[256,256]{1,0:T(8,128)S(1)} %fusion.6), channel_id=1, source_target_pairs={{0,16},{16,0},{1,17},{17,1},{2,18},{18,2},{3,19},{19,3},{4,20},{20... | collective-permute-start | bytes 786440 | tf_op jit(solution)/shard_map/ppermute | solution.py:18
  445.7 18.1 %copy-start.4 = (f32[1,8448,256]{1,2,0:T(8,128)S(1)}, f32[1,8448,256]{1,2,0:T(8,128)}, u32[]{:S(2)}) copy-start(f32[1,8448,256]{1,2,0:T(8,128)} %all-gather.14.cloned.1.call-done) | copy-start | bytes 25952260
  445.7 18.5 %copy-start.1 = (f32[8192,256]{1,0:T(8,128)S(1)}, f32[8192,256]{1,0:T(8,128)}, u32[]{:S(2)}) copy-start(f32[8192,256]{1,0:T(8,128)} %convolution_subtract_fusion.1) | copy-start | bytes 25165828
  455.3 8.5 %collective-permute-start.7 = (f32[256,256]{1,0:T(8,128)S(1)}, f32[256,256]{1,0:T(8,128)S(1)}, u32[]{:S(2)}, u32[]{:S(2)}) collective-permute-start(f32[256,256]{1,0:T(8,128)S(1)} %fusion.7), channel_id=1, source_target_pairs={{0,16},{16,0},{1,17},{17,1},{2,18},{18,2},{3,19},{19,3},{4,20},{20... | collective-permute-start | bytes 786440 | tf_op jit(solution)/shard_map/ppermute | solution.py:18
Sparse Core Ops, SparseCore 0:
  10.6 94.2 all-gather.5
  106.4 91.4 all-gather.7
  199.5 91.4 all-gather.9
  293.1 75.9 all-gather.11
  371.2 74.4 all-gather.13
